TPU v7x, 32 devices: a whole 2x2x4 slice. The times are simulated.
32 devices in a mesh: ctx: 8 (over z, core), head: 4 (over y, x).
Axes of the slice: x: 2, y: 2, z: 4, core: 2. Of those that a mesh axis runs over, the one named last changes fastest.
Arguments:
- queries: bfloat16 [2048, 8192], P(('ctx', 'head')), may hold values from -100 to 100
- keys: bfloat16 [2048, 1024], P(('ctx', 'head')), may hold values from -100 to 100
- values: bfloat16 [2048, 1024], P(('ctx', 'head')), may hold values from -6 to 6
- out_grad: bfloat16 [2048, 8192], P(('ctx', 'head')), may hold values from -6 to 6
- doc_ids: int32 [2048], replicated, may hold values from 0 to 3, never falling along the last dimension, each value on 1 to 1024 neighbouring positions
Outputs:
- query_grad: float32 [2048, 8192], P(('ctx', 'head'))
- key_grad: float32 [2048, 1024], P(('ctx', 'head'))
- value_grad: float32 [2048, 1024], P(('ctx', 'head'))
Inputs may be any that keep to these rules, and one draw needn't show every extreme that they name: `doc_ids`: never falling along the sequence; each document holds 1 to 1024 tokens, one exactly 1024.
All inputs are finite; a program needn't handle non-finite values.
Results may differ from a plain program's by a relative error of at most 0.004.
Values may be sent and summed in bfloat16 or wider, within the bound.
A program may use at most 64 MiB of HBM per device.

v0:
```python
import jax
import jax.numpy as jnp
from jax import lax
from jax.sharding import PartitionSpec as P

HD = 128


def passed_along(array, axis, by):
    size = lax.axis_size(axis)
    pairs = [(i, i + by) for i in range(size) if 0 <= i + by < size]
    return lax.ppermute(array, axis, pairs)


def body(queries, keys, values, out_grad, doc_ids):
    head_count = lax.axis_size("head")
    row_count = queries.shape[0] * head_count
    score_scale = 1.0 / HD**0.5
    query_loc, key_loc, value_loc, grad_loc = (
        lax.all_to_all(queries, "head", split_axis=1, concat_axis=0, tiled=True),
        lax.all_to_all(keys, "head", split_axis=1, concat_axis=0, tiled=True),
        lax.all_to_all(values, "head", split_axis=1, concat_axis=0, tiled=True),
        lax.all_to_all(out_grad, "head", split_axis=1, concat_axis=0, tiled=True),
    )
    kv_local = key_loc.shape[1] // HD
    group_size = query_loc.shape[1] // key_loc.shape[1]
    key_value = jnp.stack([key_loc, value_loc])
    received = [key_value]
    current = key_value
    for stride in range(1, 4):
        current = passed_along(current, "ctx", 1)
        received.append(current)
    window_kv = jnp.concatenate(received[::-1], axis=1)
    key_win = window_kv[0].reshape(4 * row_count, kv_local, HD)
    value_win = window_kv[1].reshape(4 * row_count, kv_local, HD)
    first_row = lax.axis_index("ctx") * row_count
    query_pos = first_row + jnp.arange(row_count, dtype=jnp.int32)
    key_pos = first_row - 3 * row_count + jnp.arange(4 * row_count, dtype=jnp.int32)
    query_doc = lax.dynamic_slice_in_dim(doc_ids, first_row, row_count, 0)
    key_doc = jnp.concatenate(
        [
            lax.dynamic_slice_in_dim(
                doc_ids, jnp.maximum(first_row - stride * row_count, 0), row_count, 0
            )
            for stride in (3, 2, 1, 0)
        ],
        0,
    )
    allowed = (key_pos[None, :] <= query_pos[:, None]) & (
        key_pos[None, :] > query_pos[:, None] - 3 * row_count
    )
    allowed = allowed & (key_pos[None, :] >= 0) & (query_doc[:, None] == key_doc[None, :])
    query_heads = query_loc.reshape(row_count, kv_local, group_size, HD)
    scores = (
        jnp.einsum("ikgd,jkd->kgij", query_heads, key_win, preferred_element_type=jnp.float32)
        * score_scale
    )
    scores = jnp.where(allowed[None, None], scores, -jnp.inf)
    row_max = jnp.max(scores, -1, keepdims=True)
    expo = jnp.exp(scores - row_max)
    weights = expo / jnp.sum(expo, -1, keepdims=True)
    weight_bf = weights.astype(jnp.bfloat16)
    attended = jnp.einsum(
        "kgij,jkd->ikgd", weight_bf, value_win, preferred_element_type=jnp.float32
    )
    grad_heads = grad_loc.reshape(row_count, kv_local, group_size, HD)
    delta_sum = jnp.transpose(jnp.sum(grad_heads.astype(jnp.float32) * attended, -1), (1, 2, 0))
    value_part = jnp.einsum(
        "kgij,ikgd->jkd", weight_bf, grad_heads, preferred_element_type=jnp.float32
    )
    prob_grad = jnp.einsum(
        "ikgd,jkd->kgij", grad_heads, value_win, preferred_element_type=jnp.float32
    )
    score_grad = (weights * (prob_grad - delta_sum[..., None])).astype(jnp.bfloat16)
    query_full = (
        jnp.einsum("kgij,jkd->ikgd", score_grad, key_win, preferred_element_type=jnp.float32)
        * score_scale
    )
    key_part = (
        jnp.einsum("kgij,ikgd->jkd", score_grad, query_heads, preferred_element_type=jnp.float32)
        * score_scale
    )
    partials = jnp.stack([key_part, value_part]).reshape(2, 4 * row_count, kv_local * HD)

    def piece(stride):
        return partials[:, (3 - stride) * row_count : (4 - stride) * row_count]

    total = piece(3)
    for stride in (2, 1, 0):
        total = passed_along(total, "ctx", -1) + piece(stride)
    query_rows = query_full.reshape(row_count, -1)
    query_back, key_back, value_back = (
        lax.all_to_all(query_rows, "head", split_axis=0, concat_axis=1, tiled=True),
        lax.all_to_all(total[0], "head", split_axis=0, concat_axis=1, tiled=True),
        lax.all_to_all(total[1], "head", split_axis=0, concat_axis=1, tiled=True),
    )
    return (query_back, key_back, value_back)


def solution(mesh):
    return jax.shard_map(
        body,
        mesh=mesh,
        in_specs=(
            P(("ctx", "head"), None),
            P(("ctx", "head"), None),
            P(("ctx", "head"), None),
            P(("ctx", "head"), None),
            P(),
        ),
        out_specs=(P(("ctx", "head"), None), P(("ctx", "head"), None), P(("ctx", "head"), None)),
        check_vma=False,
    )
```

profile of v0, /device:TPU:8, one launch (start us, length us, event | category | flops | bytes accessed | tf_op | source)
XLA Modules:
  0.0 173.3 jit_solution(2294293589609892568)
XLA Ops:
  0.6 0.0 copy-start.5
  0.6 1.6 copy.114
  2.2 3.7 %all-to-all-start = ((bf16[64,4,256]{2,0,1:T(8,128)(2,1)}), bf16[64,4,256]{2,0,1:T(8,128)(2,1)S(1)}, u32[]{:S(2)}, u32[]{:S(2)}) async-start(bf16[64,4,256]{2,0,1:T(8,128)(2,1)} %bitcast.112), calls=%async_computation | async-start | bytes 262144 | tf_op jit(solution)/shard_map/all_to_all | solution.py:21
  5.9 1.6 copy.113
  7.5 3.5 %all-to-all-done = bf16[64,4,256]{2,0,1:T(8,128)(2,1)S(1)} async-done(((bf16[64,4,256]{2,0,1:T(8,128)(2,1)}), bf16[64,4,256]{2,0,1:T(8,128)(2,1)S(1)}, u32[]{:S(2)}, u32[]{:S(2)}) %all-to-all-start) | async-done | bytes 131104 | tf_op jit(solution)/shard_map/all_to_all | solution.py:21
  11.0 3.3 %all-to-all-start.1 = ((bf16[64,4,256]{2,0,1:T(8,128)(2,1)}), bf16[64,4,256]{2,0,1:T(8,128)(2,1)S(1)}, u32[]{:S(2)}, u32[]{:S(2)}) async-start(bf16[64,4,256]{2,0,1:T(8,128)(2,1)} %bitcast.111), calls=%async_computation.1 | async-start | bytes 262144 | tf_op jit(solution)/shard_map/all_to_all | solution.py:22
  14.3 2.3 %copy.112 = bf16[8,4,8,2048]{3,2,0,1:T(8,128)(2,1)} copy(bf16[8,4,8,2048]{3,2,1,0:T(8,128)(2,1)} %bitcast.128) | data formatting | bytes 2097152 | tf_op jit(solution)/shard_map/all_to_all | solution.py:20
  16.6 2.7 %all-to-all-done.1 = bf16[64,4,256]{2,0,1:T(8,128)(2,1)S(1)} async-done(((bf16[64,4,256]{2,0,1:T(8,128)(2,1)}), bf16[64,4,256]{2,0,1:T(8,128)(2,1)S(1)}, u32[]{:S(2)}, u32[]{:S(2)}) %all-to-all-start.1) | async-done | bytes 131104 | tf_op jit(solution)/shard_map/all_to_all | solution.py:22
  19.3 3.5 %all-to-all-start.2 = ((bf16[64,4,2048]{2,0,1:T(8,128)(2,1)}), bf16[64,4,2048]{2,0,1:T(8,128)(2,1)S(1)}, u32[]{:S(2)}, u32[]{:S(2)}) async-start(bf16[64,4,2048]{2,0,1:T(8,128)(2,1)} %bitcast.110), calls=%async_computation.2 | async-start | bytes 2097152 | tf_op jit(solution)/shard_map/all_to_all | solution.py:20
  22.8 1.9 %collective-permute-start = (bf16[2,256,256]{2,1,0:T(8,128)(2,1)S(1)}, bf16[2,256,256]{2,1,0:T(8,128)(2,1)S(1)}, u32[]{:S(2)}, u32[]{:S(2)}) collective-permute-start(bf16[2,256,256]{2,1,0:T(8,128)(2,1)S(1)} %pad_maximum_fusion.1), channel_id=1, source_target_pairs={{0,4},{4,8},{8,12},{12,16},{16,20},{20,24},{24,28},{1,5},{5,9},{9,... | collective-permute-start | bytes 786440 | tf_op jit(solution)/shard_map/ppermute | solution.py:12
  24.8 2.3 %copy.111 = bf16[8,4,8,2048]{3,2,0,1:T(8,128)(2,1)} copy(bf16[8,4,8,2048]{3,2,1,0:T(8,128)(2,1)} %bitcast.129) | data formatting | bytes 2097152 | tf_op jit(solution)/shard_map/all_to_all | solution.py:23
  27.1 7.0 %all-to-all-done.2 = bf16[64,4,2048]{2,0,1:T(8,128)(2,1)S(1)} async-done(((bf16[64,4,2048]{2,0,1:T(8,128)(2,1)}), bf16[64,4,2048]{2,0,1:T(8,128)(2,1)S(1)}, u32[]{:S(2)}, u32[]{:S(2)}) %all-to-all-start.2) | async-done | bytes 1048608 | tf_op jit(solution)/shard_map/all_to_all | solution.py:20
  34.1 3.5 %all-to-all-start.3 = ((bf16[64,4,2048]{2,0,1:T(8,128)(2,1)}), bf16[64,4,2048]{2,0,1:T(8,128)(2,1)S(1)}, u32[]{:S(2)}, u32[]{:S(2)}) async-start(bf16[64,4,2048]{2,0,1:T(8,128)(2,1)} %bitcast.109), calls=%async_computation.3 | async-start | bytes 2097152 | tf_op jit(solution)/shard_map/all_to_all | solution.py:23
  37.6 0.0 collective-permute-done
  37.6 0.0 copy-start.4
  37.7 1.9 %collective-permute-start.1 = (bf16[2,256,256]{2,1,0:T(8,128)(2,1)S(1)}, bf16[2,256,256]{2,1,0:T(8,128)(2,1)}, u32[]{:S(2)}, u32[]{:S(2)}) collective-permute-start(bf16[2,256,256]{2,1,0:T(8,128)(2,1)S(1)} %collective-permute-done), channel_id=1, source_target_pairs={{0,4},{4,8},{8,12},{12,16},{16,20},{20,24},{24,28},{1,5},{5,9},{9,... | collective-permute-start | bytes 786440 | tf_op jit(solution)/shard_map/ppermute | solution.py:12
  39.6 0.0 copy-done.5
  39.6 0.1 fusion.22
  39.7 5.7 %collective-permute-done.1 = bf16[2,256,256]{2,1,0:T(8,128)(2,1)} collective-permute-done((bf16[2,256,256]{2,1,0:T(8,128)(2,1)S(1)}, bf16[2,256,256]{2,1,0:T(8,128)(2,1)}, u32[]{:S(2)}, u32[]{:S(2)}) %collective-permute-start.1) | collective-permute-done | bytes 262176 | tf_op jit(solution)/shard_map/ppermute | solution.py:12
  45.4 1.9 %collective-permute-start.2 = (bf16[2,256,256]{2,1,0:T(8,128)(2,1)}, bf16[2,256,256]{2,1,0:T(8,128)(2,1)}, u32[]{:S(2)}, u32[]{:S(2)}) collective-permute-start(bf16[2,256,256]{2,1,0:T(8,128)(2,1)} %collective-permute-done.1), channel_id=1, source_target_pairs={{0,4},{4,8},{8,12},{12,16},{16,20},{20,24},{24,28},{1,5},{5,9},{9,... | collective-permute-start | bytes 786440 | tf_op jit(solution)/shard_map/ppermute | solution.py:12
  47.4 1.5 compare_and_fusion
  48.9 0.0 copy-done.4
  48.9 0.2 copy.105
  49.2 0.8 copy.77
  50.0 0.0 copy-start.1
  50.0 0.8 all-to-all-done.3
  50.7 1.2 copy.106
  51.9 1.7 copy.71
  53.6 0.0 collective-permute-done.2
  53.6 1.2 maximum_maximum_fusion
  54.8 1.0 fusion.20
  55.9 1.2 copy.67
  57.1 2.1 %copy.63 = bf16[1,1024,256]{1,2,0:T(8,128)(2,1)} copy(bf16[1,1024,256]{2,1,0:T(8,128)(2,1)} %get-tuple-element.4) | data formatting | bytes 1048576 | tf_op jit(solution)/shard_map/slice | solution.py:34
  59.2 9.6 %fusion.23 = (f32[2,8,256]{2,1,0:T(8,128)S(1)}, f32[2,8,256,1024]{2,3,1,0:T(8,128)}) fusion(pred[256,1024]{0,1:T(8,128)(4,1)S(1)} %copy-done.3, bf16[1024,2,128,1]{0,2,3,1:T(8,128)(2,1)} %bitcast.122, bf16[256,2,8,128]{0,3,2,1:T(8,128)(2,1)S(1)} %copy.77), kind=kOutput, calls=%fused_computation.48 | convolution fusion | flops 1090520064 | bytes 18628608 | tf_op jit(solution)/shard_map/sub | solution.py:60
  68.8 6.6 %fusion.7 = bf16[2,8,256,1024]{2,3,1,0:T(8,128)(2,1)S(1)} fusion(f32[2,8,256,1024]{2,3,1,0:T(8,128)} %get-tuple-element.13, f32[2,8,256]{2,1,0:T(8,128)S(1)} %get-tuple-element.12), kind=kLoop, calls=%fused_computation.11 | loop fusion | flops 8388608 | bytes 25182208 | tf_op jit(solution)/shard_map/convert_element_type | solution.py:62
  75.4 3.8 %fusion.24 = f32[2,1024,128,1]{1,2,3,0:T(8,128)} fusion(bf16[2,8,256,1024]{2,3,1,0:T(8,128)(2,1)S(1)} %fusion.7, bf16[256,2,8,128]{0,3,2,1:T(8,128)(2,1)S(1)} %copy.71), kind=kOutput, calls=%fused_computation.49 | convolution fusion | flops 1073741824 | bytes 10485760 | tf_op jit(solution)/shard_map/kgij,ikgd->jkd/dot_general | solution.py:68
  79.2 1.3 fusion.8
  80.5 1.6 copy.81
  82.1 7.1 %fusion.2 = bf16[2,8,256,1024]{2,3,1,0:T(8,128)(2,1)S(1)} fusion(f32[2,8,256]{2,1,0:T(8,128)S(1)} %bitcast.137, f32[2,8,256,1024]{2,3,1,0:T(8,128)} %get-tuple-element.13, f32[2,8,256]{2,1,0:T(8,128)S(1)} %get-tuple-element.12, bf16[1024,2,128,1]{0,2,3,1:T(8,128)(2,1)S(1)} %bitcast.120, bf16[256,2,8,128]{0,3,2,1:T(8,128)(2,1)S(1)} %copy.71), kind=kOutput, calls=%fused_computation.3 | convolution fusion | flops 1090519040 | bytes 26771456 | tf_op jit(solution)/shard_map/ikgd,jkd->kgij/dot_general | solution.py:71
  89.2 0.0 copy-start
  89.2 3.2 %copy-done = bf16[2,8,256,1024]{2,3,1,0:T(8,128)(2,1)} copy-done((bf16[2,8,256,1024]{2,3,1,0:T(8,128)(2,1)}, bf16[2,8,256,1024]{2,3,1,0:T(8,128)(2,1)S(1)}, u32[]{:S(2)}) %copy-start) | copy-done | bytes 8388632
  92.5 5.1 %fusion.11 = f32[2,1024,128]{1,2,0:T(8,128)} fusion(bf16[2,8,256,1024]{2,3,1,0:T(8,128)(2,1)S(1)} %fusion.2, bf16[256,2,8,128]{0,3,2,1:T(8,128)(2,1)} %copy-done.1), kind=kOutput, calls=%fused_computation.23 | convolution fusion | flops 1074003968 | bytes 10485760 | tf_op jit(solution)/shard_map/kgij,ikgd->jkd/dot_general | solution.py:80
  97.6 1.6 copy.80
  99.2 3.0 %collective-permute-start.3 = (f32[2,256,256]{2,1,0:T(8,128)S(1)}, f32[2,256,256]{2,1,0:T(8,128)S(1)}, u32[]{:S(2)}, u32[]{:S(2)}) collective-permute-start(f32[2,256,256]{2,1,0:T(8,128)S(1)} %fusion.14), channel_id=1, source_target_pairs={{4,0},{8,4},{12,8},{16,12},{20,16},{24,20},{28,24},{5,1},{9,5},{13... | collective-permute-start | bytes 1572872 | tf_op jit(solution)/shard_map/ppermute | solution.py:12
  102.1 6.7 %collective-permute-done.3 = f32[2,256,256]{2,1,0:T(8,128)S(1)} collective-permute-done((f32[2,256,256]{2,1,0:T(8,128)S(1)}, f32[2,256,256]{2,1,0:T(8,128)S(1)}, u32[]{:S(2)}, u32[]{:S(2)}) %collective-permute-start.3) | collective-permute-done | bytes 524320 | tf_op jit(solution)/shard_map/ppermute | solution.py:12
  108.8 0.9 fusion.16
  109.8 4.0 %collective-permute-start.4 = (f32[2,256,256]{2,1,0:T(8,128)}, f32[2,256,256]{2,1,0:T(8,128)}, u32[]{:S(2)}, u32[]{:S(2)}) collective-permute-start(f32[2,256,256]{2,1,0:T(8,128)} %fusion.16), channel_id=1, source_target_pairs={{4,0},{8,4},{12,8},{16,12},{20,16},{24,20},{28,24},{5,1},{9,5},{13... | collective-permute-start | bytes 1572872 | tf_op jit(solution)/shard_map/ppermute | solution.py:12
  113.8 6.0 %multiply_bitcast_fusion = f32[256,2,8,128]{0,3,2,1:T(8,128)} fusion(bf16[1024,2,128,1]{0,2,3,1:T(8,128)(2,1)S(1)} %bitcast.123, bf16[2,8,256,1024]{2,3,1,0:T(8,128)(2,1)} %copy-done), kind=kOutput, calls=%fused_computation.20 | convolution fusion | flops 1074266112 | bytes 11010048 | tf_op jit(solution)/shard_map/kgij,jkd->ikgd/dot_general | solution.py:76
  119.8 3.0 %copy.74 = f32[256,2,8,128]{3,2,1,0:T(8,128)} copy(f32[256,2,8,128]{0,3,2,1:T(8,128)} %multiply_bitcast_fusion) | data formatting | bytes 4194304 | tf_op jit(solution)/shard_map/mul | solution.py:76
  122.8 2.7 %all_to_all.102 = f32[4,64,2048]{2,1,0:T(8,128)} reshape(f32[256,2,8,128]{3,2,1,0:T(8,128)} %copy.74) | data formatting | bytes 4194304 | tf_op jit(solution)/shard_map/all_to_all | solution.py:93
  125.5 4.5 %all-to-all-start.4 = ((f32[4,64,2048]{2,1,0:T(8,128)}), f32[4,64,2048]{2,1,0:T(8,128)}, u32[]{:S(2)}, u32[]{:S(2)}) async-start(f32[4,64,2048]{2,1,0:T(8,128)} %all_to_all.102), calls=%async_computation.4 | async-start | bytes 4194304 | tf_op jit(solution)/shard_map/all_to_all | solution.py:93
  130.0 0.0 collective-permute-done.4
  130.0 1.1 fusion.13
  131.1 1.9 %collective-permute-start.5 = (f32[2,256,256]{2,1,0:T(8,128)S(1)}, f32[2,256,256]{2,1,0:T(8,128)S(1)}, u32[]{:S(2)}, u32[]{:S(2)}) collective-permute-start(f32[2,256,256]{2,1,0:T(8,128)S(1)} %fusion.13), channel_id=1, source_target_pairs={{4,0},{8,4},{12,8},{16,12},{20,16},{24,20},{28,24},{5,1},{9,5},{13... | collective-permute-start | bytes 1572872 | tf_op jit(solution)/shard_map/ppermute | solution.py:12
  133.0 6.7 %collective-permute-done.5 = f32[2,256,256]{2,1,0:T(8,128)S(1)} collective-permute-done((f32[2,256,256]{2,1,0:T(8,128)S(1)}, f32[2,256,256]{2,1,0:T(8,128)S(1)}, u32[]{:S(2)}, u32[]{:S(2)}) %collective-permute-start.5) | collective-permute-done | bytes 524320 | tf_op jit(solution)/shard_map/ppermute | solution.py:12
  139.7 0.1 fusion.17
  139.8 0.7 fusion.21
  140.5 15.0 %all-to-all-done.4 = f32[4,64,2048]{2,1,0:T(8,128)} async-done(((f32[4,64,2048]{2,1,0:T(8,128)}), f32[4,64,2048]{2,1,0:T(8,128)}, u32[]{:S(2)}, u32[]{:S(2)}) %all-to-all-start.4) | async-done | bytes 2097184 | tf_op jit(solution)/shard_map/all_to_all | solution.py:93
  155.5 8.3 %all_to_all.121 = f32[4,64,256]{2,1,0:T(8,128)S(1)} all-to-all(f32[4,64,256]{2,1,0:T(8,128)S(1)} %bitcast.132), channel_id=1, replica_groups=mesh['ctx'=8,'head'=4] {'head'}, dimensions={0} | all-to-all | bytes 524288 | tf_op jit(solution)/shard_map/all_to_all | solution.py:94
  163.8 3.4 %all-to-all-start.6 = ((f32[4,64,256]{2,1,0:T(8,128)}), f32[4,64,256]{2,1,0:T(8,128)S(1)}, u32[]{:S(2)}, u32[]{:S(2)}) async-start(f32[4,64,256]{2,1,0:T(8,128)} %bitcast.30), calls=%async_computation.6 | async-start | bytes 524288 | tf_op jit(solution)/shard_map/all_to_all | solution.py:95
  167.2 3.1 %copy.102 = f32[4,8,8,2048]{3,2,0,1:T(8,128)} copy(f32[4,8,8,2048]{3,2,1,0:T(8,128)} %bitcast.53) | data formatting | bytes 4194304 | tf_op jit(solution)/shard_map/all_to_all | solution.py:93
  170.3 0.7 copy.103
  171.1 1.5 all-to-all-done.6
  172.5 0.7 copy.104
  (10 shorter events, 0.1 us)
Async XLA Ops:
  0.6 39.0 %copy-start.5 = (s32[2048]{0:T(1024)S(1)}, s32[2048]{0:T(1024)}, u32[]{:S(2)}) copy-start(s32[2048]{0:T(1024)} %param.9) | copy-start | bytes 24580
  2.2 8.7 %all-to-all-start = ((bf16[64,4,256]{2,0,1:T(8,128)(2,1)}), bf16[64,4,256]{2,0,1:T(8,128)(2,1)S(1)}, u32[]{:S(2)}, u32[]{:S(2)}) async-start(bf16[64,4,256]{2,0,1:T(8,128)(2,1)} %bitcast.112), calls=%async_computation | async-start | bytes 262144 | tf_op jit(solution)/shard_map/all_to_all | solution.py:21
  11.0 8.3 %all-to-all-start.1 = ((bf16[64,4,256]{2,0,1:T(8,128)(2,1)}), bf16[64,4,256]{2,0,1:T(8,128)(2,1)S(1)}, u32[]{:S(2)}, u32[]{:S(2)}) async-start(bf16[64,4,256]{2,0,1:T(8,128)(2,1)} %bitcast.111), calls=%async_computation.1 | async-start | bytes 262144 | tf_op jit(solution)/shard_map/all_to_all | solution.py:22
  19.3 14.8 %all-to-all-start.2 = ((bf16[64,4,2048]{2,0,1:T(8,128)(2,1)}), bf16[64,4,2048]{2,0,1:T(8,128)(2,1)S(1)}, u32[]{:S(2)}, u32[]{:S(2)}) async-start(bf16[64,4,2048]{2,0,1:T(8,128)(2,1)} %bitcast.110), calls=%async_computation.2 | async-start | bytes 2097152 | tf_op jit(solution)/shard_map/all_to_all | solution.py:20
  22.8 14.8 %collective-permute-start = (bf16[2,256,256]{2,1,0:T(8,128)(2,1)S(1)}, bf16[2,256,256]{2,1,0:T(8,128)(2,1)S(1)}, u32[]{:S(2)}, u32[]{:S(2)}) collective-permute-start(bf16[2,256,256]{2,1,0:T(8,128)(2,1)S(1)} %pad_maximum_fusion.1), channel_id=1, source_target_pairs={{0,4},{4,8},{8,12},{12,16},{16,20},{20,24},{24,28},{1,5},{5,9},{9,... | collective-permute-start | bytes 786440 | tf_op jit(solution)/shard_map/ppermute | solution.py:12
  34.1 16.6 %all-to-all-start.3 = ((bf16[64,4,2048]{2,0,1:T(8,128)(2,1)}), bf16[64,4,2048]{2,0,1:T(8,128)(2,1)S(1)}, u32[]{:S(2)}, u32[]{:S(2)}) async-start(bf16[64,4,2048]{2,0,1:T(8,128)(2,1)} %bitcast.109), calls=%async_computation.3 | async-start | bytes 2097152 | tf_op jit(solution)/shard_map/all_to_all | solution.py:23
  37.6 11.3 %copy-start.4 = (bf16[2,256,256]{2,1,0:T(8,128)(2,1)}, bf16[2,256,256]{2,1,0:T(8,128)(2,1)S(1)}, u32[]{:S(2)}) copy-start(bf16[2,256,256]{2,1,0:T(8,128)(2,1)S(1)} %collective-permute-done) | copy-start | bytes 786436
  37.7 7.8 %collective-permute-start.1 = (bf16[2,256,256]{2,1,0:T(8,128)(2,1)S(1)}, bf16[2,256,256]{2,1,0:T(8,128)(2,1)}, u32[]{:S(2)}, u32[]{:S(2)}) collective-permute-start(bf16[2,256,256]{2,1,0:T(8,128)(2,1)S(1)} %collective-permute-done), channel_id=1, source_target_pairs={{0,4},{4,8},{8,12},{12,16},{16,20},{20,24},{24,28},{1,5},{5,9},{9,... | collective-permute-start | bytes 786440 | tf_op jit(solution)/shard_map/ppermute | solution.py:12
  45.4 8.2 %collective-permute-start.2 = (bf16[2,256,256]{2,1,0:T(8,128)(2,1)}, bf16[2,256,256]{2,1,0:T(8,128)(2,1)}, u32[]{:S(2)}, u32[]{:S(2)}) collective-permute-start(bf16[2,256,256]{2,1,0:T(8,128)(2,1)} %collective-permute-done.1), channel_id=1, source_target_pairs={{0,4},{4,8},{8,12},{12,16},{16,20},{20,24},{24,28},{1,5},{5,9},{9,... | collective-permute-start | bytes 786440 | tf_op jit(solution)/shard_map/ppermute | solution.py:12
  50.0 18.8 %copy-start.1 = (bf16[256,2,8,128]{0,3,2,1:T(8,128)(2,1)}, bf16[256,2,8,128]{0,3,2,1:T(8,128)(2,1)S(1)}, u32[]{:S(2)}) copy-start(bf16[256,2,8,128]{0,3,2,1:T(8,128)(2,1)S(1)} %copy.77) | copy-start | bytes 3145732
  51.9 7.2 %copy-start.3 = (pred[256,1024]{0,1:T(8,128)(4,1)S(1)}, pred[256,1024]{0,1:T(8,128)(4,1)}, u32[]{:S(2)}) copy-start(pred[256,1024]{0,1:T(8,128)(4,1)} %compare_and_fusion) | copy-start | bytes 786436
  89.2 3.2 %copy-start = (bf16[2,8,256,1024]{2,3,1,0:T(8,128)(2,1)}, bf16[2,8,256,1024]{2,3,1,0:T(8,128)(2,1)S(1)}, u32[]{:S(2)}) copy-start(bf16[2,8,256,1024]{2,3,1,0:T(8,128)(2,1)S(1)} %fusion.2) | copy-start | bytes 25165828
  92.5 21.3 %copy-start.2 = (bf16[1,1024,256]{1,2,0:T(8,128)(2,1)S(1)}, bf16[1,1024,256]{1,2,0:T(8,128)(2,1)}, u32[]{:S(2)}) copy-start(bf16[1,1024,256]{1,2,0:T(8,128)(2,1)} %copy.63) | copy-start | bytes 1572868
  99.2 9.7 %collective-permute-start.3 = (f32[2,256,256]{2,1,0:T(8,128)S(1)}, f32[2,256,256]{2,1,0:T(8,128)S(1)}, u32[]{:S(2)}, u32[]{:S(2)}) collective-permute-start(f32[2,256,256]{2,1,0:T(8,128)S(1)} %fusion.14), channel_id=1, source_target_pairs={{4,0},{8,4},{12,8},{16,12},{20,16},{24,20},{28,24},{5,1},{9,5},{13... | collective-permute-start | bytes 1572872 | tf_op jit(solution)/shard_map/ppermute | solution.py:12
  109.8 20.2 %collective-permute-start.4 = (f32[2,256,256]{2,1,0:T(8,128)}, f32[2,256,256]{2,1,0:T(8,128)}, u32[]{:S(2)}, u32[]{:S(2)}) collective-permute-start(f32[2,256,256]{2,1,0:T(8,128)} %fusion.16), channel_id=1, source_target_pairs={{4,0},{8,4},{12,8},{16,12},{20,16},{24,20},{28,24},{5,1},{9,5},{13... | collective-permute-start | bytes 1572872 | tf_op jit(solution)/shard_map/ppermute | solution.py:12
  125.5 30.0 %all-to-all-start.4 = ((f32[4,64,2048]{2,1,0:T(8,128)}), f32[4,64,2048]{2,1,0:T(8,128)}, u32[]{:S(2)}, u32[]{:S(2)}) async-start(f32[4,64,2048]{2,1,0:T(8,128)} %all_to_all.102), calls=%async_computation.4 | async-start | bytes 4194304 | tf_op jit(solution)/shard_map/all_to_all | solution.py:93
  131.1 8.6 %collective-permute-start.5 = (f32[2,256,256]{2,1,0:T(8,128)S(1)}, f32[2,256,256]{2,1,0:T(8,128)S(1)}, u32[]{:S(2)}, u32[]{:S(2)}) collective-permute-start(f32[2,256,256]{2,1,0:T(8,128)S(1)} %fusion.13), channel_id=1, source_target_pairs={{4,0},{8,4},{12,8},{16,12},{20,16},{24,20},{28,24},{5,1},{9,5},{13... | collective-permute-start | bytes 1572872 | tf_op jit(solution)/shard_map/ppermute | solution.py:12
  163.8 8.8 %all-to-all-start.6 = ((f32[4,64,256]{2,1,0:T(8,128)}), f32[4,64,256]{2,1,0:T(8,128)S(1)}, u32[]{:S(2)}, u32[]{:S(2)}) async-start(f32[4,64,256]{2,1,0:T(8,128)} %bitcast.30), calls=%async_computation.6 | async-start | bytes 524288 | tf_op jit(solution)/shard_map/all_to_all | solution.py:95
where the time goes:
time: 175 us; the launch traced here: 173 us
  waiting for transfers between devices  49.4 us (28%)
  starting transfers between devices  36.6 us (21%)
  local copies, waits for them, and re-layouts  33.5 us (19%)
  matrix products  32.9 us (19%)
  other arithmetic  11.6 us (7%)
  blocking collectives  8.28 us (5%)
    ppermute x6, waiting for transfers between devices, passed_along(): return lax.ppermute(array, axis, pairs)  19.1 us
    all_to_all x1, waiting for transfers between devices, body(): lax.all_to_all(query_rows, 'head', split_axis=0, concat_axis=1, tiled=True)  15 us
    ppermute x6, starting transfers between devices, passed_along(): return lax.ppermute(array, axis, pairs)  14.6 us
    sub x1, matrix products, body(): expo = jnp.exp(scores - row_max)  9.64 us
    all_to_all x1, blocking collectives, body(): lax.all_to_all(total[0], 'head', split_axis=0, concat_axis=1, tiled=True)  8.28 us
    dot_general x1, matrix products, body(): jnp.einsum('ikgd,jkd->kgij', grad_heads, value_win, preferred_element_typ...  7.12 us
    all_to_all x1, waiting for transfers between devices, body(): lax.all_to_all(queries, 'head', split_axis=1, concat_axis=0, tiled=True)  7.03 us
    convert_element_type x1, other arithmetic, body(): weight_bf = weights.astype(jnp.bfloat16)  6.62 us
  transfers between devices with their start and end apart: 12, of which 9 were waited for; matrix products, arithmetic and copies ran while one was open for 15% of the time, Pallas kernels for 0%

commit v1 on v0

--- a/solution.py
+++ b/solution.py
@@ -2,8 +2,12 @@
 import jax.numpy as jnp
 from jax import lax
 from jax.sharding import PartitionSpec as P
+from jax.lax import all_to_all, psum
 
 HD = 128
+lift_kinds = lambda field: jnp.concatenate(
+    all_to_all(jnp.stack(jnp.split(field, psum(1, "head"), 0)), "head", 0, 0), 1
+)
 
 
 def passed_along(array, axis, by):
@@ -91,7 +95,7 @@
     query_rows = query_full.reshape(row_count, -1)
     query_back, key_back, value_back = (
         lax.all_to_all(query_rows, "head", split_axis=0, concat_axis=1, tiled=True),
-        lax.all_to_all(total[0], "head", split_axis=0, concat_axis=1, tiled=True),
+        lift_kinds(total[0]),
         lax.all_to_all(total[1], "head", split_axis=0, concat_axis=1, tiled=True),
     )
     return (query_back, key_back, value_back)

time: 175 us -> 165 us (0.943)
  blocking collectives: 8.28 us -> 0 us
  waiting for transfers between devices: 49.4 us -> 43.1 us
  starting transfers between devices: 36.6 us -> 40.4 us
    all_to_all x1, waiting for transfers between devices: 15 us -> 4.02 us  [body(): lax.all_to_all(query_rows, 'head', split_axis=0, concat_axis=1, tiled=True)]
    all_to_all x1 -> x0, blocking collectives: 8.28 us -> none  [body(): lax.all_to_all(total[0], 'head', split_axis=0, concat_axis=1, tiled=True)]
    all_to_all x0 -> x1, starting transfers between devices: none -> 3.41 us  [all_to_all(jnp.stack(jnp.split(field, psum(1, 'head'), 0)), 'head', 0, 0)]
    all_to_all x1, waiting for transfers between devices: 1.48 us -> 4.59 us  [body(): lax.all_to_all(total[1], 'head', split_axis=0, concat_axis=1, tiled=True)]
  transfers between devices with their start and end apart: 12 -> 13, of which waited for: 9 -> 10; matrix products, arithmetic and copies ran while one was open for 15% -> 17% of each run, Pallas kernels for 0% -> 0%
where the time goes in v1:
time: 165 us; the launch traced here: 163 us
  waiting for transfers between devices  43.1 us (26%)
  starting transfers between devices  40.4 us (24%)
  local copies, waits for them, and re-layouts  33.5 us (20%)
  matrix products  32.9 us (20%)
  other arithmetic  12.3 us (7%)
    ppermute x6, waiting for transfers between devices, passed_along(): return lax.ppermute(array, axis, pairs)  19.1 us
    ppermute x6, starting transfers between devices, passed_along(): return lax.ppermute(array, axis, pairs)  15 us
    sub x1, matrix products, body(): expo = jnp.exp(scores - row_max)  9.62 us
    dot_general x1, matrix products, body(): jnp.einsum('ikgd,jkd->kgij', grad_heads, value_win, preferred_element_typ...  7.11 us
    all_to_all x1, waiting for transfers between devices, body(): lax.all_to_all(queries, 'head', split_axis=1, concat_axis=0, tiled=True)  7.03 us
    convert_element_type x1, other arithmetic, body(): weight_bf = weights.astype(jnp.bfloat16)  6.62 us
    dot_general x1, matrix products, body(): jnp.einsum('kgij,jkd->ikgd', score_grad, key_win, preferred_element_type=...  6 us
    all_to_all x2, local copies, waits for them, and re-layouts, body(): lax.all_to_all(query_rows, 'head', split_axis=0, concat_axis=1, tiled=True)  5.84 us
  transfers between devices with their start and end apart: 13, of which 10 were waited for; matrix products, arithmetic and copies ran while one was open for 17% of the time, Pallas kernels for 0%

profile of v1, /device:TPU:8, one launch (start us, length us, event | category | flops | bytes accessed | tf_op | source)
XLA Modules:
  0.0 163.1 jit_solution(17773292918229964597)
XLA Ops:
  0.6 0.0 copy-start.5
  0.6 1.6 copy.114
  2.2 3.7 %all-to-all-start = ((bf16[64,4,256]{2,0,1:T(8,128)(2,1)}), bf16[64,4,256]{2,0,1:T(8,128)(2,1)S(1)}, u32[]{:S(2)}, u32[]{:S(2)}) async-start(bf16[64,4,256]{2,0,1:T(8,128)(2,1)} %bitcast.111), calls=%async_computation | async-start | bytes 262144 | tf_op jit(solution)/shard_map/all_to_all | solution.py:25
  5.9 1.6 copy.113
  7.5 3.5 %all-to-all-done = bf16[64,4,256]{2,0,1:T(8,128)(2,1)S(1)} async-done(((bf16[64,4,256]{2,0,1:T(8,128)(2,1)}), bf16[64,4,256]{2,0,1:T(8,128)(2,1)S(1)}, u32[]{:S(2)}, u32[]{:S(2)}) %all-to-all-start) | async-done | bytes 131104 | tf_op jit(solution)/shard_map/all_to_all | solution.py:25
  11.0 3.3 %all-to-all-start.1 = ((bf16[64,4,256]{2,0,1:T(8,128)(2,1)}), bf16[64,4,256]{2,0,1:T(8,128)(2,1)S(1)}, u32[]{:S(2)}, u32[]{:S(2)}) async-start(bf16[64,4,256]{2,0,1:T(8,128)(2,1)} %bitcast.110), calls=%async_computation.1 | async-start | bytes 262144 | tf_op jit(solution)/shard_map/all_to_all | solution.py:26
  14.3 2.3 %copy.112 = bf16[8,4,8,2048]{3,2,0,1:T(8,128)(2,1)} copy(bf16[8,4,8,2048]{3,2,1,0:T(8,128)(2,1)} %bitcast.127) | data formatting | bytes 2097152 | tf_op jit(solution)/shard_map/all_to_all | solution.py:24
  16.6 2.7 %all-to-all-done.1 = bf16[64,4,256]{2,0,1:T(8,128)(2,1)S(1)} async-done(((bf16[64,4,256]{2,0,1:T(8,128)(2,1)}), bf16[64,4,256]{2,0,1:T(8,128)(2,1)S(1)}, u32[]{:S(2)}, u32[]{:S(2)}) %all-to-all-start.1) | async-done | bytes 131104 | tf_op jit(solution)/shard_map/all_to_all | solution.py:26
  19.3 3.5 %all-to-all-start.2 = ((bf16[64,4,2048]{2,0,1:T(8,128)(2,1)}), bf16[64,4,2048]{2,0,1:T(8,128)(2,1)S(1)}, u32[]{:S(2)}, u32[]{:S(2)}) async-start(bf16[64,4,2048]{2,0,1:T(8,128)(2,1)} %bitcast.109), calls=%async_computation.2 | async-start | bytes 2097152 | tf_op jit(solution)/shard_map/all_to_all | solution.py:24
  22.8 1.9 %collective-permute-start = (bf16[2,256,256]{2,1,0:T(8,128)(2,1)S(1)}, bf16[2,256,256]{2,1,0:T(8,128)(2,1)S(1)}, u32[]{:S(2)}, u32[]{:S(2)}) collective-permute-start(bf16[2,256,256]{2,1,0:T(8,128)(2,1)S(1)} %pad_maximum_fusion.1), channel_id=1, source_target_pairs={{0,4},{4,8},{8,12},{12,16},{16,20},{20,24},{24,28},{1,5},{5,9},{9,... | collective-permute-start | bytes 786440 | tf_op jit(solution)/shard_map/ppermute | solution.py:16
  24.8 2.3 %copy.111 = bf16[8,4,8,2048]{3,2,0,1:T(8,128)(2,1)} copy(bf16[8,4,8,2048]{3,2,1,0:T(8,128)(2,1)} %bitcast.128) | data formatting | bytes 2097152 | tf_op jit(solution)/shard_map/all_to_all | solution.py:27
  27.1 7.0 %all-to-all-done.2 = bf16[64,4,2048]{2,0,1:T(8,128)(2,1)S(1)} async-done(((bf16[64,4,2048]{2,0,1:T(8,128)(2,1)}), bf16[64,4,2048]{2,0,1:T(8,128)(2,1)S(1)}, u32[]{:S(2)}, u32[]{:S(2)}) %all-to-all-start.2) | async-done | bytes 1048608 | tf_op jit(solution)/shard_map/all_to_all | solution.py:24
  34.1 3.5 %all-to-all-start.3 = ((bf16[64,4,2048]{2,0,1:T(8,128)(2,1)}), bf16[64,4,2048]{2,0,1:T(8,128)(2,1)S(1)}, u32[]{:S(2)}, u32[]{:S(2)}) async-start(bf16[64,4,2048]{2,0,1:T(8,128)(2,1)} %bitcast.108), calls=%async_computation.3 | async-start | bytes 2097152 | tf_op jit(solution)/shard_map/all_to_all | solution.py:27
  37.6 0.0 collective-permute-done
  37.6 0.0 copy-start.4
  37.7 1.9 %collective-permute-start.1 = (bf16[2,256,256]{2,1,0:T(8,128)(2,1)S(1)}, bf16[2,256,256]{2,1,0:T(8,128)(2,1)}, u32[]{:S(2)}, u32[]{:S(2)}) collective-permute-start(bf16[2,256,256]{2,1,0:T(8,128)(2,1)S(1)} %collective-permute-done), channel_id=1, source_target_pairs={{0,4},{4,8},{8,12},{12,16},{16,20},{20,24},{24,28},{1,5},{5,9},{9,... | collective-permute-start | bytes 786440 | tf_op jit(solution)/shard_map/ppermute | solution.py:16
  39.6 0.0 copy-done.5
  39.6 0.1 fusion.22
  39.7 5.7 %collective-permute-done.1 = bf16[2,256,256]{2,1,0:T(8,128)(2,1)} collective-permute-done((bf16[2,256,256]{2,1,0:T(8,128)(2,1)S(1)}, bf16[2,256,256]{2,1,0:T(8,128)(2,1)}, u32[]{:S(2)}, u32[]{:S(2)}) %collective-permute-start.1) | collective-permute-done | bytes 262176 | tf_op jit(solution)/shard_map/ppermute | solution.py:16
  45.4 1.9 %collective-permute-start.2 = (bf16[2,256,256]{2,1,0:T(8,128)(2,1)}, bf16[2,256,256]{2,1,0:T(8,128)(2,1)}, u32[]{:S(2)}, u32[]{:S(2)}) collective-permute-start(bf16[2,256,256]{2,1,0:T(8,128)(2,1)} %collective-permute-done.1), channel_id=1, source_target_pairs={{0,4},{4,8},{8,12},{12,16},{16,20},{20,24},{24,28},{1,5},{5,9},{9,... | collective-permute-start | bytes 786440 | tf_op jit(solution)/shard_map/ppermute | solution.py:16
  47.4 1.5 compare_and_fusion
  48.9 0.2 copy.105
  49.2 0.8 copy.77
  50.0 0.8 all-to-all-done.3
  50.7 1.2 copy.106
  51.9 1.7 %copy.71 = bf16[256,2,8,128]{0,3,2,1:T(8,128)(2,1)S(1)} copy(bf16[256,2,8,128]{3,2,1,0:T(8,128)(2,1)} %bitcast.117) | data formatting | bytes 2097152 | tf_op jit(solution)/shard_map/reshape | solution.py:70
  53.6 0.0 collective-permute-done.2
  53.6 1.2 maximum_maximum_fusion
  54.8 1.0 fusion.20
  55.9 1.2 copy.67
  57.1 2.1 %copy.63 = bf16[1,1024,256]{1,2,0:T(8,128)(2,1)} copy(bf16[1,1024,256]{2,1,0:T(8,128)(2,1)} %get-tuple-element.4) | data formatting | bytes 1048576 | tf_op jit(solution)/shard_map/slice | solution.py:38
  59.2 9.6 %fusion.23 = (f32[2,8,256]{2,1,0:T(8,128)S(1)}, f32[2,8,256,1024]{2,3,1,0:T(8,128)}) fusion(pred[256,1024]{0,1:T(8,128)(4,1)S(1)} %copy-done.3, bf16[1024,2,128,1]{0,2,3,1:T(8,128)(2,1)} %bitcast.121, bf16[256,2,8,128]{0,3,2,1:T(8,128)(2,1)S(1)} %copy.77), kind=kOutput, calls=%fused_computation.49 | convolution fusion | flops 1090520064 | bytes 18628608 | tf_op jit(solution)/shard_map/sub | solution.py:64
  68.8 6.6 %fusion.7 = bf16[2,8,256,1024]{2,3,1,0:T(8,128)(2,1)S(1)} fusion(f32[2,8,256,1024]{2,3,1,0:T(8,128)} %get-tuple-element.15, f32[2,8,256]{2,1,0:T(8,128)S(1)} %get-tuple-element.14), kind=kLoop, calls=%fused_computation.11 | loop fusion | flops 8388608 | bytes 25182208 | tf_op jit(solution)/shard_map/convert_element_type | solution.py:66
  75.4 3.8 %fusion.24 = f32[2,1024,128,1]{1,2,3,0:T(8,128)} fusion(bf16[2,8,256,1024]{2,3,1,0:T(8,128)(2,1)S(1)} %fusion.7, bf16[256,2,8,128]{0,3,2,1:T(8,128)(2,1)S(1)} %copy.71), kind=kOutput, calls=%fused_computation.50 | convolution fusion | flops 1073741824 | bytes 10485760 | tf_op jit(solution)/shard_map/kgij,ikgd->jkd/dot_general | solution.py:72
  79.2 1.3 fusion.8
  80.5 1.6 copy.81
  82.1 7.1 %fusion.2 = bf16[2,8,256,1024]{2,3,1,0:T(8,128)(2,1)S(1)} fusion(f32[2,8,256]{2,1,0:T(8,128)S(1)} %bitcast.135, f32[2,8,256,1024]{2,3,1,0:T(8,128)} %get-tuple-element.15, f32[2,8,256]{2,1,0:T(8,128)S(1)} %get-tuple-element.14, bf16[1024,2,128,1]{0,2,3,1:T(8,128)(2,1)S(1)} %bitcast.119, bf16[256,2,8,128]{0,3,2,1:T(8,128)(2,1)S(1)} %copy.71), kind=kOutput, calls=%fused_computation.3 | convolution fusion | flops 1090519040 | bytes 26771456 | tf_op jit(solution)/shard_map/ikgd,jkd->kgij/dot_general | solution.py:75
  89.2 3.2 %copy-done = bf16[2,8,256,1024]{2,3,1,0:T(8,128)(2,1)} copy-done((bf16[2,8,256,1024]{2,3,1,0:T(8,128)(2,1)}, bf16[2,8,256,1024]{2,3,1,0:T(8,128)(2,1)S(1)}, u32[]{:S(2)}) %copy-start) | copy-done | bytes 8388632
  92.5 5.1 %fusion.11 = f32[2,1024,128]{1,2,0:T(8,128)} fusion(bf16[2,8,256,1024]{2,3,1,0:T(8,128)(2,1)S(1)} %fusion.2, bf16[256,2,8,128]{0,3,2,1:T(8,128)(2,1)} %copy-done.1), kind=kOutput, calls=%fused_computation.23 | convolution fusion | flops 1074003968 | bytes 10485760 | tf_op jit(solution)/shard_map/kgij,ikgd->jkd/dot_general | solution.py:84
  97.5 1.6 copy.80
  99.1 0.9 fusion.14
  100.0 3.1 %collective-permute-start.3 = (f32[2,256,256]{2,1,0:T(8,128)}, f32[2,256,256]{2,1,0:T(8,128)}, u32[]{:S(2)}, u32[]{:S(2)}) collective-permute-start(f32[2,256,256]{2,1,0:T(8,128)} %fusion.14), channel_id=1, source_target_pairs={{4,0},{8,4},{12,8},{16,12},{20,16},{24,20},{28,24},{5,1},{9,5},{13... | collective-permute-start | bytes 1572872 | tf_op jit(solution)/shard_map/ppermute | solution.py:16
  103.2 6.0 %multiply_bitcast_fusion = f32[256,2,8,128]{0,3,2,1:T(8,128)} fusion(bf16[1024,2,128,1]{0,2,3,1:T(8,128)(2,1)S(1)} %bitcast.122, bf16[2,8,256,1024]{2,3,1,0:T(8,128)(2,1)} %copy-done), kind=kOutput, calls=%fused_computation.20 | convolution fusion | flops 1074266112 | bytes 11010048 | tf_op jit(solution)/shard_map/kgij,jkd->ikgd/dot_general | solution.py:80
  109.2 3.0 %copy.74 = f32[256,2,8,128]{3,2,1,0:T(8,128)} copy(f32[256,2,8,128]{0,3,2,1:T(8,128)} %multiply_bitcast_fusion) | data formatting | bytes 4194304 | tf_op jit(solution)/shard_map/mul | solution.py:80
  112.2 2.7 %all_to_all.91 = f32[4,64,2048]{2,1,0:T(8,128)} reshape(f32[256,2,8,128]{3,2,1,0:T(8,128)} %copy.74) | data formatting | bytes 4194304 | tf_op jit(solution)/shard_map/all_to_all | solution.py:97
  114.9 4.5 %all-to-all-start.4 = ((f32[4,64,2048]{2,1,0:T(8,128)}), f32[4,64,2048]{2,1,0:T(8,128)}, u32[]{:S(2)}, u32[]{:S(2)}) async-start(f32[4,64,2048]{2,1,0:T(8,128)} %all_to_all.91), calls=%async_computation.4 | async-start | bytes 4194304 | tf_op jit(solution)/shard_map/all_to_all | solution.py:97
  119.3 0.0 collective-permute-done.3
  119.4 1.1 fusion.16
  120.5 1.9 %collective-permute-start.4 = (f32[2,256,256]{2,1,0:T(8,128)S(1)}, f32[2,256,256]{2,1,0:T(8,128)S(1)}, u32[]{:S(2)}, u32[]{:S(2)}) collective-permute-start(f32[2,256,256]{2,1,0:T(8,128)S(1)} %fusion.16), channel_id=1, source_target_pairs={{4,0},{8,4},{12,8},{16,12},{20,16},{24,20},{28,24},{5,1},{9,5},{13... | collective-permute-start | bytes 1572872 | tf_op jit(solution)/shard_map/ppermute | solution.py:16
  122.4 6.7 %collective-permute-done.4 = f32[2,256,256]{2,1,0:T(8,128)S(1)} collective-permute-done((f32[2,256,256]{2,1,0:T(8,128)S(1)}, f32[2,256,256]{2,1,0:T(8,128)S(1)}, u32[]{:S(2)}, u32[]{:S(2)}) %collective-permute-start.4) | collective-permute-done | bytes 524320 | tf_op jit(solution)/shard_map/ppermute | solution.py:16
  129.1 0.1 fusion.13
  129.2 4.2 %collective-permute-start.5 = (f32[2,256,256]{2,1,0:T(8,128)S(1)}, f32[2,256,256]{2,1,0:T(8,128)S(1)}, u32[]{:S(2)}, u32[]{:S(2)}) collective-permute-start(f32[2,256,256]{2,1,0:T(8,128)S(1)} %fusion.13), channel_id=1, source_target_pairs={{4,0},{8,4},{12,8},{16,12},{20,16},{24,20},{28,24},{5,1},{9,5},{13... | collective-permute-start | bytes 1572872 | tf_op jit(solution)/shard_map/ppermute | solution.py:16
  133.4 6.7 %collective-permute-done.5 = f32[2,256,256]{2,1,0:T(8,128)S(1)} collective-permute-done((f32[2,256,256]{2,1,0:T(8,128)S(1)}, f32[2,256,256]{2,1,0:T(8,128)S(1)}, u32[]{:S(2)}, u32[]{:S(2)}) %collective-permute-start.5) | collective-permute-done | bytes 524320 | tf_op jit(solution)/shard_map/ppermute | solution.py:16
  140.1 0.1 fusion.17
  140.1 0.7 slice.45
  140.9 4.0 %all-to-all-done.4 = f32[4,64,2048]{2,1,0:T(8,128)} async-done(((f32[4,64,2048]{2,1,0:T(8,128)}), f32[4,64,2048]{2,1,0:T(8,128)}, u32[]{:S(2)}, u32[]{:S(2)}) %all-to-all-start.4) | async-done | bytes 2097184 | tf_op jit(solution)/shard_map/all_to_all | solution.py:97
  144.9 3.4 %all-to-all-start.6 = ((f32[4,64,256]{2,1,0:T(8,128)}), f32[4,64,256]{2,1,0:T(8,128)S(1)}, u32[]{:S(2)}, u32[]{:S(2)}) async-start(f32[4,64,256]{2,1,0:T(8,128)} %bitcast.29), calls=%async_computation.6 | async-start | bytes 524288 | tf_op jit(solution)/shard_map/all_to_all | solution.py:99
  148.3 0.7 pad_maximum_fusion.2
  149.1 4.6 %all-to-all-done.6 = f32[4,64,256]{2,1,0:T(8,128)S(1)} async-done(((f32[4,64,256]{2,1,0:T(8,128)}), f32[4,64,256]{2,1,0:T(8,128)S(1)}, u32[]{:S(2)}, u32[]{:S(2)}) %all-to-all-start.6) | async-done | bytes 262176 | tf_op jit(solution)/shard_map/all_to_all | solution.py:99
  153.6 3.4 %all-to-all-start.5 = ((f32[4,64,256]{2,1,0:T(8,128)}), f32[4,64,256]{2,1,0:T(8,128)S(1)}, u32[]{:S(2)}, u32[]{:S(2)}) async-start(f32[4,64,256]{2,1,0:T(8,128)} %pad_maximum_fusion.2), calls=%async_computation.5 | async-start | bytes 524288 | tf_op jit(solution)/shard_map/all_to_all | solution.py:9
  157.1 3.1 %copy.102 = f32[4,8,8,2048]{3,2,0,1:T(8,128)} copy(f32[4,8,8,2048]{3,2,1,0:T(8,128)} %bitcast.52) | data formatting | bytes 4194304 | tf_op jit(solution)/shard_map/all_to_all | solution.py:97
  160.2 0.7 copy.104
  160.9 1.5 all-to-all-done.5
  162.4 0.7 copy.103
  (13 shorter events, 0.1 us)
Async XLA Ops:
  0.6 39.0 %copy-start.5 = (s32[2048]{0:T(1024)S(1)}, s32[2048]{0:T(1024)}, u32[]{:S(2)}) copy-start(s32[2048]{0:T(1024)} %param.9) | copy-start | bytes 24580
  2.2 8.7 %all-to-all-start = ((bf16[64,4,256]{2,0,1:T(8,128)(2,1)}), bf16[64,4,256]{2,0,1:T(8,128)(2,1)S(1)}, u32[]{:S(2)}, u32[]{:S(2)}) async-start(bf16[64,4,256]{2,0,1:T(8,128)(2,1)} %bitcast.111), calls=%async_computation | async-start | bytes 262144 | tf_op jit(solution)/shard_map/all_to_all | solution.py:25
  11.0 8.3 %all-to-all-start.1 = ((bf16[64,4,256]{2,0,1:T(8,128)(2,1)}), bf16[64,4,256]{2,0,1:T(8,128)(2,1)S(1)}, u32[]{:S(2)}, u32[]{:S(2)}) async-start(bf16[64,4,256]{2,0,1:T(8,128)(2,1)} %bitcast.110), calls=%async_computation.1 | async-start | bytes 262144 | tf_op jit(solution)/shard_map/all_to_all | solution.py:26
  19.3 14.8 %all-to-all-start.2 = ((bf16[64,4,2048]{2,0,1:T(8,128)(2,1)}), bf16[64,4,2048]{2,0,1:T(8,128)(2,1)S(1)}, u32[]{:S(2)}, u32[]{:S(2)}) async-start(bf16[64,4,2048]{2,0,1:T(8,128)(2,1)} %bitcast.109), calls=%async_computation.2 | async-start | bytes 2097152 | tf_op jit(solution)/shard_map/all_to_all | solution.py:24
  22.8 14.8 %collective-permute-start = (bf16[2,256,256]{2,1,0:T(8,128)(2,1)S(1)}, bf16[2,256,256]{2,1,0:T(8,128)(2,1)S(1)}, u32[]{:S(2)}, u32[]{:S(2)}) collective-permute-start(bf16[2,256,256]{2,1,0:T(8,128)(2,1)S(1)} %pad_maximum_fusion.1), channel_id=1, source_target_pairs={{0,4},{4,8},{8,12},{12,16},{16,20},{20,24},{24,28},{1,5},{5,9},{9,... | collective-permute-start | bytes 786440 | tf_op jit(solution)/shard_map/ppermute | solution.py:16
  34.1 16.6 %all-to-all-start.3 = ((bf16[64,4,2048]{2,0,1:T(8,128)(2,1)}), bf16[64,4,2048]{2,0,1:T(8,128)(2,1)S(1)}, u32[]{:S(2)}, u32[]{:S(2)}) async-start(bf16[64,4,2048]{2,0,1:T(8,128)(2,1)} %bitcast.108), calls=%async_computation.3 | async-start | bytes 2097152 | tf_op jit(solution)/shard_map/all_to_all | solution.py:27
  37.6 11.3 %copy-start.4 = (bf16[2,256,256]{2,1,0:T(8,128)(2,1)}, bf16[2,256,256]{2,1,0:T(8,128)(2,1)S(1)}, u32[]{:S(2)}) copy-start(bf16[2,256,256]{2,1,0:T(8,128)(2,1)S(1)} %collective-permute-done) | copy-start | bytes 786436
  37.7 7.8 %collective-permute-start.1 = (bf16[2,256,256]{2,1,0:T(8,128)(2,1)S(1)}, bf16[2,256,256]{2,1,0:T(8,128)(2,1)}, u32[]{:S(2)}, u32[]{:S(2)}) collective-permute-start(bf16[2,256,256]{2,1,0:T(8,128)(2,1)S(1)} %collective-permute-done), channel_id=1, source_target_pairs={{0,4},{4,8},{8,12},{12,16},{16,20},{20,24},{24,28},{1,5},{5,9},{9,... | collective-permute-start | bytes 786440 | tf_op jit(solution)/shard_map/ppermute | solution.py:16
  45.4 8.2 %collective-permute-start.2 = (bf16[2,256,256]{2,1,0:T(8,128)(2,1)}, bf16[2,256,256]{2,1,0:T(8,128)(2,1)}, u32[]{:S(2)}, u32[]{:S(2)}) collective-permute-start(bf16[2,256,256]{2,1,0:T(8,128)(2,1)} %collective-permute-done.1), channel_id=1, source_target_pairs={{0,4},{4,8},{8,12},{12,16},{16,20},{20,24},{24,28},{1,5},{5,9},{9,... | collective-permute-start | bytes 786440 | tf_op jit(solution)/shard_map/ppermute | solution.py:16
  50.0 18.8 %copy-start.1 = (bf16[256,2,8,128]{0,3,2,1:T(8,128)(2,1)}, bf16[256,2,8,128]{0,3,2,1:T(8,128)(2,1)S(1)}, u32[]{:S(2)}) copy-start(bf16[256,2,8,128]{0,3,2,1:T(8,128)(2,1)S(1)} %copy.77) | copy-start | bytes 3145732
  51.9 7.2 %copy-start.3 = (pred[256,1024]{0,1:T(8,128)(4,1)S(1)}, pred[256,1024]{0,1:T(8,128)(4,1)}, u32[]{:S(2)}) copy-start(pred[256,1024]{0,1:T(8,128)(4,1)} %compare_and_fusion) | copy-start | bytes 786436
  89.2 3.3 %copy-start = (bf16[2,8,256,1024]{2,3,1,0:T(8,128)(2,1)}, bf16[2,8,256,1024]{2,3,1,0:T(8,128)(2,1)S(1)}, u32[]{:S(2)}) copy-start(bf16[2,8,256,1024]{2,3,1,0:T(8,128)(2,1)S(1)} %fusion.2) | copy-start | bytes 25165828
  92.5 10.7 %copy-start.2 = (bf16[1,1024,256]{1,2,0:T(8,128)(2,1)S(1)}, bf16[1,1024,256]{1,2,0:T(8,128)(2,1)}, u32[]{:S(2)}) copy-start(bf16[1,1024,256]{1,2,0:T(8,128)(2,1)} %copy.63) | copy-start | bytes 1572868
  100.0 19.4 %collective-permute-start.3 = (f32[2,256,256]{2,1,0:T(8,128)}, f32[2,256,256]{2,1,0:T(8,128)}, u32[]{:S(2)}, u32[]{:S(2)}) collective-permute-start(f32[2,256,256]{2,1,0:T(8,128)} %fusion.14), channel_id=1, source_target_pairs={{4,0},{8,4},{12,8},{16,12},{20,16},{24,20},{28,24},{5,1},{9,5},{13... | collective-permute-start | bytes 1572872 | tf_op jit(solution)/shard_map/ppermute | solution.py:16
  114.9 30.0 %all-to-all-start.4 = ((f32[4,64,2048]{2,1,0:T(8,128)}), f32[4,64,2048]{2,1,0:T(8,128)}, u32[]{:S(2)}, u32[]{:S(2)}) async-start(f32[4,64,2048]{2,1,0:T(8,128)} %all_to_all.91), calls=%async_computation.4 | async-start | bytes 4194304 | tf_op jit(solution)/shard_map/all_to_all | solution.py:97
  120.5 8.6 %collective-permute-start.4 = (f32[2,256,256]{2,1,0:T(8,128)S(1)}, f32[2,256,256]{2,1,0:T(8,128)S(1)}, u32[]{:S(2)}, u32[]{:S(2)}) collective-permute-start(f32[2,256,256]{2,1,0:T(8,128)S(1)} %fusion.16), channel_id=1, source_target_pairs={{4,0},{8,4},{12,8},{16,12},{20,16},{24,20},{28,24},{5,1},{9,5},{13... | collective-permute-start | bytes 1572872 | tf_op jit(solution)/shard_map/ppermute | solution.py:16
  129.2 10.9 %collective-permute-start.5 = (f32[2,256,256]{2,1,0:T(8,128)S(1)}, f32[2,256,256]{2,1,0:T(8,128)S(1)}, u32[]{:S(2)}, u32[]{:S(2)}) collective-permute-start(f32[2,256,256]{2,1,0:T(8,128)S(1)} %fusion.13), channel_id=1, source_target_pairs={{4,0},{8,4},{12,8},{16,12},{20,16},{24,20},{28,24},{5,1},{9,5},{13... | collective-permute-start | bytes 1572872 | tf_op jit(solution)/shard_map/ppermute | solution.py:16
  144.9 8.8 %all-to-all-start.6 = ((f32[4,64,256]{2,1,0:T(8,128)}), f32[4,64,256]{2,1,0:T(8,128)S(1)}, u32[]{:S(2)}, u32[]{:S(2)}) async-start(f32[4,64,256]{2,1,0:T(8,128)} %bitcast.29), calls=%async_computation.6 | async-start | bytes 524288 | tf_op jit(solution)/shard_map/all_to_all | solution.py:99
  153.6 8.8 %all-to-all-start.5 = ((f32[4,64,256]{2,1,0:T(8,128)}), f32[4,64,256]{2,1,0:T(8,128)S(1)}, u32[]{:S(2)}, u32[]{:S(2)}) async-start(f32[4,64,256]{2,1,0:T(8,128)} %pad_maximum_fusion.2), calls=%async_computation.5 | async-start | bytes 524288 | tf_op jit(solution)/shard_map/all_to_all | solution.py:9
